TPU v7x, 32 devices: a whole 2x2x4 slice. The times are simulated.
32 devices in a mesh: gx: 2 (over y), gy: 4 (over x, core), gz: 4 (over z).
Axes of the slice: x: 2, y: 2, z: 4, core: 2. Of those that a mesh axis runs over, the one named last changes fastest.
Arguments:
- density: float32 [32, 64, 4096], P('gx', 'gy', 'gz'), may hold values from -19 to 19
Outputs:
- potential: float32 [32, 64, 4096], P('gx', 'gy', 'gz')
- coulomb: float32 [64, 64], replicated
All inputs are finite; a program needn't handle non-finite values.
Results may differ from a plain program's by a relative error of at most 0.000057.
Values sent between devices are 32-bit elements; how exact they have to be, the bound alone decides.
No kernel may reach another device: no remote copies, remote signals or barrier semaphores. Data moves between devices by JAX's collectives and lax.ppermute only.
A program may use at most 64 MiB of HBM per device.

v0:
```python
import jax
import jax.numpy as jnp
from jax import lax
from jax.sharding import PartitionSpec as P

PAIRS = 64
LEVELS = 6
COARSE_SWEEPS = 8
OMEGA = 2.0 / 3.0


def extended_2(x, sides, width):
    for axis, dim in sides:
        size, length = (lax.axis_size(axis), x.shape[dim])
        up = [(i, (i + 1) % size) for i in range(size - 1)]
        down = [(j, i) for i, j in up]
        last = lax.slice_in_dim(x, length - width, length, axis=dim)
        initial = lax.slice_in_dim(x, 0, width, axis=dim)
        before = lax.ppermute(last, axis, up)
        after = lax.ppermute(initial, axis, down)
        x = jnp.concatenate([before, x, after], axis=dim)
    return x


def neighbours(padded):
    total = padded[2:, 1:-1, 1:-1] + padded[:-2, 1:-1, 1:-1]
    total = total + padded[1:-1, 2:, 1:-1] + padded[1:-1, :-2, 1:-1]
    return total + padded[1:-1, 1:-1, 2:] + padded[1:-1, 1:-1, :-2]


def apply_inner(padded, factor):
    return factor * (6.0 * padded[1:-1, 1:-1, 1:-1] - neighbours(padded))


def sweep_inner(padded, source, factor):
    return padded[1:-1, 1:-1, 1:-1] + OMEGA * (source - apply_inner(padded, factor)) / (
        6.0 * factor
    )


def zero_rim(current):
    return jnp.pad(current, ((1, 1), (1, 1), (1, 1), (0, 0)))


def restrict(residual):
    size_x, size_y, size_z, count = residual.shape
    grouped = residual.reshape(size_x // 2, 2, size_y // 2, 2, size_z // 2, 2, count)
    return jnp.mean(grouped, axis=(1, 3, 5))


def prolong(correction):
    return jnp.repeat(jnp.repeat(jnp.repeat(correction, 2, axis=0), 2, axis=1), 2, axis=2)


def global_cycle(source, grid_level):
    factor = 0.25 ** (grid_level - 1)
    current = OMEGA * source / (6.0 * factor)
    if grid_level == LEVELS:
        for repeat_no in range(COARSE_SWEEPS - 1):
            current = sweep_inner(zero_rim(current), source, factor)
        return current
    current = sweep_inner(zero_rim(current), source, factor)
    residual = source - apply_inner(zero_rim(current), factor)
    current = current + prolong(global_cycle(restrict(residual), grid_level + 1))
    for repeat_no in range(2):
        current = sweep_inner(zero_rim(current), source, factor)
    return current


def arrange(stacked, block_shape):
    size_x, size_y, size_z, count = block_shape
    devs_x, devs_y, devs_z = (lax.axis_size("gx"), lax.axis_size("gy"), lax.axis_size("gz"))
    grouped = stacked.reshape(devs_x, devs_y, devs_z, size_x, size_y, size_z, count)
    grouped = grouped.transpose(0, 3, 1, 4, 2, 5, 6)
    return grouped.reshape(devs_x * size_x, devs_y * size_y, devs_z * size_z, count)


def own_block(gathered, block_shape):
    size_x, size_y, size_z, count = block_shape
    starts = (
        lax.axis_index("gx") * size_x,
        lax.axis_index("gy") * size_y,
        lax.axis_index("gz") * size_z,
        jnp.int32(0),
    )
    return lax.dynamic_slice(gathered, starts, block_shape)


def edge_mask(length, where, devices):
    position = jnp.arange(length + 2, dtype=jnp.int32) - 1 + where * length
    return (position >= 0) & (position < length * devices)


def inside_mask(block_shape):
    mask_x = edge_mask(block_shape[0], lax.axis_index("gx"), lax.axis_size("gx"))
    mask_y = edge_mask(block_shape[1], lax.axis_index("gy"), lax.axis_size("gy"))
    mask_z = edge_mask(block_shape[2], lax.axis_index("gz"), lax.axis_size("gz"))
    joined = mask_x[:, None, None] & mask_y[None, :, None] & mask_z[None, None, :]
    return joined[..., None].astype(jnp.float32)


def double_sweep(current, source, factor):
    count = current.shape[3]
    extended = extended_2(
        jnp.concatenate([current, source], axis=3), (("gx", 0), ("gy", 1), ("gz", 2)), 2
    )
    source_wide = extended[1:-1, 1:-1, 1:-1, count:]
    swept = sweep_inner(extended[..., :count], source_wide, factor) * inside_mask(current.shape)
    return swept


def distributed(source, grid_level):
    factor = 0.25 ** (grid_level - 1)
    if grid_level == LEVELS - 1:
        stacked = lax.all_gather(source[None], ("gx", "gy", "gz"), axis=0, tiled=True)
        return own_block(global_cycle(arrange(stacked, source.shape), grid_level), source.shape)
    current = OMEGA * source / (6.0 * factor)
    swept = double_sweep(current, source, factor)
    residual = source - apply_inner(swept, factor)
    current = swept[1:-1, 1:-1, 1:-1]
    current = current + prolong(distributed(restrict(residual), grid_level + 1))
    current = sweep_inner(double_sweep(current, source, factor), source, factor)
    return current


def local(density):
    cells_x, cells_y, merged = density.shape
    cells_z = merged // PAIRS
    cells = density.reshape(cells_x, cells_y, cells_z, PAIRS)
    solved = distributed(cells, 1)
    partial_block = jnp.dot(
        cells.reshape(-1, PAIRS).T,
        solved.reshape(-1, PAIRS),
        precision=lax.Precision.HIGHEST,
        preferred_element_type=jnp.float32,
    )
    summed = lax.psum(partial_block, ("gx", "gy", "gz"))
    total_cells = (
        cells_x
        * cells_y
        * cells_z
        * lax.axis_size("gx")
        * lax.axis_size("gy")
        * lax.axis_size("gz")
    )
    coulomb = summed * (4.0 / total_cells)
    return (solved.reshape(cells_x, cells_y, merged), coulomb)


def solution(mesh):
    return jax.shard_map(
        local,
        mesh=mesh,
        in_specs=(P("gx", "gy", "gz"),),
        out_specs=(P("gx", "gy", "gz"), P()),
        check_vma=False,
    )
```

profile of v0, /device:TPU:14, one launch (start us, length us, event | category | flops | bytes accessed | tf_op | source)
XLA Modules:
  0.0 362.6 jit_solution(3952595412670936373)
XLA Ops:
  6.1 4.6 %collective-permute-start.1 = (f32[2,16,16,128]{3,2,1,0:T(8,128)S(1)}, f32[2,16,16,128]{3,2,1,0:T(8,128)S(1)}, u32[]{:S(2)}, u32[]{:S(2)}) collective-permute-start(f32[2,16,16,128]{3,2,1,0:T(8,128)S(1)} %get-tuple-element.10), channel_id=1, source_target_pairs={{16,0},{17,1},{18,2},{19,3},{20,4},{21,5},{22,6},{23,7},{24,8},{25... | collective-permute-start | bytes 786440 | tf_op jit(solution)/shard_map/ppermute | solution.py:20
  10.7 4.0 %collective-permute-done = f32[2,16,16,128]{3,2,1,0:T(8,128)S(1)} collective-permute-done((f32[2,16,16,128]{3,2,1,0:T(8,128)S(1)}, f32[2,16,16,128]{3,2,1,0:T(8,128)S(1)}, u32[]{:S(2)}, u32[]{:S(2)}) %collective-permute-start) | collective-permute-done | bytes 262176 | tf_op jit(solution)/shard_map/ppermute | solution.py:19
  15.9 2.2 fusion.55
  20.1 3.6 %collective-permute-start.3 = (f32[20,2,16,128]{3,2,1,0:T(8,128)S(1)}, f32[20,2,16,128]{3,2,1,0:T(8,128)S(1)}, u32[]{:S(2)}, u32[]{:S(2)}) collective-permute-start(f32[20,2,16,128]{3,2,1,0:T(8,128)S(1)} %get-tuple-element.19), channel_id=1, source_target_pairs={{4,0},{8,4},{12,8},{5,1},{9,5},{13,9},{6,2},{10,6},{14,10},{7,3},{... | collective-permute-start | bytes 983048 | tf_op jit(solution)/shard_map/ppermute | solution.py:20
  23.9 2.7 collective-permute-done.2
  29.3 3.5 collective-permute-start.4
  32.8 2.4 collective-permute-start.5
  35.4 3.8 %collective-permute-done.4 = f32[20,20,2,128]{3,2,1,0:T(2,128)S(1)} collective-permute-done((f32[20,20,2,128]{3,2,1,0:T(2,128)S(1)}, f32[20,20,2,128]{3,2,1,0:T(2,128)S(1)}, u32[]{:S(2)}, u32[]{:S(2)}) %collective-permute-start.4) | collective-permute-done | bytes 409632 | tf_op jit(solution)/shard_map/ppermute | solution.py:19
  39.2 3.5 collective-permute-done.5
  42.7 3.2 fusion.5
  45.9 8.6 %fusion.23 = f32[18,18,18,64]{3,2,1,0:T(8,128)S(1)} fusion(f32[16,16,16,64]{3,2,1,0:T(8,128)S(1)} %reshape.351, f32[20,20,2,128]{3,2,1,0:T(2,128)S(1)} %collective-permute-done.4, f32[20,2,16,128]{3,2,1,0:T(8,128)S(1)} %collective-permute-done.3, f32[20,2,16,128]{3,2,1,0:T(8,128)S(1)} %collective-permute-done.2, ...), kind=kLoop, calls=%fused_computation.29 | loop fusion | flops 8584704 | bytes 14570272 | tf_op jit(solution)/shard_map/mul | solution.py:108
  54.5 2.6 fusion.63
  57.1 3.0 reduce_sum.52
  62.2 4.5 %collective-permute-start.7 = (f32[2,8,8,128]{3,2,1,0:T(8,128)S(1)}, f32[2,8,8,128]{3,2,1,0:T(8,128)S(1)}, u32[]{:S(2)}, u32[]{:S(2)}) collective-permute-start(f32[2,8,8,128]{3,2,1,0:T(8,128)S(1)} %get-tuple-element.8), channel_id=1, source_target_pairs={{16,0},{17,1},{18,2},{19,3},{20,4},{21,5},{22,6},{23,7},{24,8},{25... | collective-permute-start | bytes 196616 | tf_op jit(solution)/shard_map/ppermute | solution.py:20
  70.7 3.6 %collective-permute-start.9 = (f32[12,2,8,128]{3,2,1,0:T(8,128)S(1)}, f32[12,2,8,128]{3,2,1,0:T(8,128)S(1)}, u32[]{:S(2)}, u32[]{:S(2)}) collective-permute-start(f32[12,2,8,128]{3,2,1,0:T(8,128)S(1)} %get-tuple-element.30), channel_id=1, source_target_pairs={{4,0},{8,4},{12,8},{5,1},{9,5},{13,9},{6,2},{10,6},{14,10},{7,3},{... | collective-permute-start | bytes 294920 | tf_op jit(solution)/shard_map/ppermute | solution.py:20
  76.8 3.5 collective-permute-start.10
  80.3 2.4 collective-permute-start.11
  83.9 3.5 collective-permute-done.11
  91.2 4.7 %collective-permute-start.13 = (f32[2,4,4,128]{3,2,1,0:T(4,128)S(1)}, f32[2,4,4,128]{3,2,1,0:T(4,128)S(1)}, u32[]{:S(2)}, u32[]{:S(2)}) collective-permute-start(f32[2,4,4,128]{3,2,1,0:T(4,128)S(1)} %get-tuple-element.47), channel_id=1, source_target_pairs={{16,0},{17,1},{18,2},{19,3},{20,4},{21,5},{22,6},{23,7},{24,8},{25... | collective-permute-start | bytes 49160 | tf_op jit(solution)/shard_map/ppermute | solution.py:20
  99.2 3.6 %collective-permute-start.15 = (f32[8,2,4,128]{3,2,1,0:T(4,128)S(1)}, f32[8,2,4,128]{3,2,1,0:T(4,128)S(1)}, u32[]{:S(2)}, u32[]{:S(2)}) collective-permute-start(f32[8,2,4,128]{3,2,1,0:T(4,128)S(1)} %get-tuple-element.45), channel_id=1, source_target_pairs={{4,0},{8,4},{12,8},{5,1},{9,5},{13,9},{6,2},{10,6},{14,10},{7,3},{... | collective-permute-start | bytes 98312 | tf_op jit(solution)/shard_map/ppermute | solution.py:20
  106.5 3.9 %collective-permute-start.17 = (f32[8,8,2,128]{3,2,1,0:T(2,128)S(1)}, f32[8,8,2,128]{3,2,1,0:T(2,128)S(1)}, u32[]{:S(2)}, u32[]{:S(2)}) collective-permute-start(f32[8,8,2,128]{3,2,1,0:T(2,128)S(1)} %get-tuple-element.38), channel_id=1, source_target_pairs={{1,0},{2,1},{3,2},{5,4},{6,5},{7,6},{9,8},{10,9},{11,10},{13,12},{... | collective-permute-start | bytes 196616 | tf_op jit(solution)/shard_map/ppermute | solution.py:20
  114.4 4.5 %collective-permute-start.19 = (f32[2,2,2,128]{3,2,1,0:T(2,128)S(1)}, f32[2,2,2,128]{3,2,1,0:T(2,128)S(1)}, u32[]{:S(2)}, u32[]{:S(2)}) collective-permute-start(f32[2,2,2,128]{3,2,1,0:T(2,128)S(1)} %pad_maximum_fusion.46), channel_id=1, source_target_pairs={{16,0},{17,1},{18,2},{19,3},{20,4},{21,5},{22,6},{23,7},{24,8},{25... | collective-permute-start | bytes 12296 | tf_op jit(solution)/shard_map/ppermute | solution.py:20
  122.3 3.6 %collective-permute-start.21 = (f32[6,2,2,128]{3,2,1,0:T(2,128)S(1)}, f32[6,2,2,128]{3,2,1,0:T(2,128)S(1)}, u32[]{:S(2)}, u32[]{:S(2)}) collective-permute-start(f32[6,2,2,128]{3,2,1,0:T(2,128)S(1)} %fusion.281), channel_id=1, source_target_pairs={{4,0},{8,4},{12,8},{5,1},{9,5},{13,9},{6,2},{10,6},{14,10},{7,3},{... | collective-permute-start | bytes 36872 | tf_op jit(solution)/shard_map/ppermute | solution.py:20
  129.9 3.9 %collective-permute-start.23 = (f32[6,6,2,128]{3,2,1,0:T(2,128)}, f32[6,6,2,128]{3,2,1,0:T(2,128)}, u32[]{:S(2)}, u32[]{:S(2)}) collective-permute-start(f32[6,6,2,128]{3,2,1,0:T(2,128)} %fusion.211), channel_id=1, source_target_pairs={{1,0},{2,1},{3,2},{5,4},{6,5},{7,6},{9,8},{10,9},{11,10},{13,12},{... | collective-permute-start | bytes 110600 | tf_op jit(solution)/shard_map/ppermute | solution.py:20
  138.5 42.3 %all-reduce.11 = f32[2048]{0:T(1024)S(1)} all-reduce(f32[2048]{0:T(1024)S(1)} %multiply_dynamic-update-slice_fusion), channel_id=2, replica_groups=mesh['gx'=2,'gy'=4,'gz'=4] {'gx','gy','gz'}, use_global_device_ids=true, to_apply=%add.11 | all-reduce | flops 2048 | bytes 16384
  183.3 4.5 %collective-permute-start.25 = (f32[2,2,2,128]{3,2,1,0:T(2,128)S(1)}, f32[2,2,2,128]{3,2,1,0:T(2,128)S(1)}, u32[]{:S(2)}, u32[]{:S(2)}) collective-permute-start(f32[2,2,2,128]{3,2,1,0:T(2,128)S(1)} %pad_maximum_fusion.47), channel_id=1, source_target_pairs={{16,0},{17,1},{18,2},{19,3},{20,4},{21,5},{22,6},{23,7},{24,8},{25... | collective-permute-start | bytes 12296 | tf_op jit(solution)/shard_map/ppermute | solution.py:20
  191.2 3.6 %collective-permute-start.27 = (f32[6,2,2,128]{3,2,1,0:T(2,128)S(1)}, f32[6,2,2,128]{3,2,1,0:T(2,128)S(1)}, u32[]{:S(2)}, u32[]{:S(2)}) collective-permute-start(f32[6,2,2,128]{3,2,1,0:T(2,128)S(1)} %fusion.283), channel_id=1, source_target_pairs={{4,0},{8,4},{12,8},{5,1},{9,5},{13,9},{6,2},{10,6},{14,10},{7,3},{... | collective-permute-start | bytes 36872 | tf_op jit(solution)/shard_map/ppermute | solution.py:20
  196.3 2.5 collective-permute-start.28
  198.8 3.3 collective-permute-start.29
  202.1 2.6 collective-permute-done.29
  206.4 4.5 %collective-permute-start.31 = (f32[2,4,4,128]{3,2,1,0:T(4,128)S(1)}, f32[2,4,4,128]{3,2,1,0:T(4,128)S(1)}, u32[]{:S(2)}, u32[]{:S(2)}) collective-permute-start(f32[2,4,4,128]{3,2,1,0:T(4,128)S(1)} %get-tuple-element.43), channel_id=1, source_target_pairs={{16,0},{17,1},{18,2},{19,3},{20,4},{21,5},{22,6},{23,7},{24,8},{25... | collective-permute-start | bytes 49160 | tf_op jit(solution)/shard_map/ppermute | solution.py:20
  214.4 3.6 %collective-permute-start.33 = (f32[8,2,4,128]{3,2,1,0:T(4,128)S(1)}, f32[8,2,4,128]{3,2,1,0:T(4,128)S(1)}, u32[]{:S(2)}, u32[]{:S(2)}) collective-permute-start(f32[8,2,4,128]{3,2,1,0:T(4,128)S(1)} %get-tuple-element.41), channel_id=1, source_target_pairs={{4,0},{8,4},{12,8},{5,1},{9,5},{13,9},{6,2},{10,6},{14,10},{7,3},{... | collective-permute-start | bytes 98312 | tf_op jit(solution)/shard_map/ppermute | solution.py:20
  221.7 3.9 %collective-permute-start.35 = (f32[8,8,2,128]{3,2,1,0:T(2,128)S(1)}, f32[8,8,2,128]{3,2,1,0:T(2,128)S(1)}, u32[]{:S(2)}, u32[]{:S(2)}) collective-permute-start(f32[8,8,2,128]{3,2,1,0:T(2,128)S(1)} %get-tuple-element.36), channel_id=1, source_target_pairs={{1,0},{2,1},{3,2},{5,4},{6,5},{7,6},{9,8},{10,9},{11,10},{13,12},{... | collective-permute-start | bytes 196616 | tf_op jit(solution)/shard_map/ppermute | solution.py:20
  230.5 4.5 %collective-permute-start.37 = (f32[2,8,8,128]{3,2,1,0:T(8,128)S(1)}, f32[2,8,8,128]{3,2,1,0:T(8,128)S(1)}, u32[]{:S(2)}, u32[]{:S(2)}) collective-permute-start(f32[2,8,8,128]{3,2,1,0:T(8,128)S(1)} %get-tuple-element.32), channel_id=1, source_target_pairs={{16,0},{17,1},{18,2},{19,3},{20,4},{21,5},{22,6},{23,7},{24,8},{25... | collective-permute-start | bytes 196616 | tf_op jit(solution)/shard_map/ppermute | solution.py:20
  239.1 3.6 %collective-permute-start.39 = (f32[12,2,8,128]{3,2,1,0:T(8,128)S(1)}, f32[12,2,8,128]{3,2,1,0:T(8,128)S(1)}, u32[]{:S(2)}, u32[]{:S(2)}) collective-permute-start(f32[12,2,8,128]{3,2,1,0:T(8,128)S(1)} %get-tuple-element.28), channel_id=1, source_target_pairs={{4,0},{8,4},{12,8},{5,1},{9,5},{13,9},{6,2},{10,6},{14,10},{7,3},{... | collective-permute-start | bytes 294920 | tf_op jit(solution)/shard_map/ppermute | solution.py:20
  247.1 3.9 %collective-permute-start.41 = (f32[12,12,2,128]{3,2,1,0:T(2,128)S(1)}, f32[12,12,2,128]{3,2,1,0:T(2,128)S(1)}, u32[]{:S(2)}, u32[]{:S(2)}) collective-permute-start(f32[12,12,2,128]{3,2,1,0:T(2,128)S(1)} %get-tuple-element.23), channel_id=1, source_target_pairs={{1,0},{2,1},{3,2},{5,4},{6,5},{7,6},{9,8},{10,9},{11,10},{13,12},{... | collective-permute-start | bytes 442376 | tf_op jit(solution)/shard_map/ppermute | solution.py:20
  260.1 4.6 %collective-permute-start.43 = (f32[2,16,16,128]{3,2,1,0:T(8,128)S(1)}, f32[2,16,16,128]{3,2,1,0:T(8,128)S(1)}, u32[]{:S(2)}, u32[]{:S(2)}) collective-permute-start(f32[2,16,16,128]{3,2,1,0:T(8,128)S(1)} %get-tuple-element.21), channel_id=1, source_target_pairs={{16,0},{17,1},{18,2},{19,3},{20,4},{21,5},{22,6},{23,7},{24,8},{25... | collective-permute-start | bytes 786440 | tf_op jit(solution)/shard_map/ppermute | solution.py:20
  264.7 2.4 collective-permute-done.42
  271.2 3.6 %collective-permute-start.45 = (f32[20,2,16,128]{3,2,1,0:T(8,128)S(1)}, f32[20,2,16,128]{3,2,1,0:T(8,128)S(1)}, u32[]{:S(2)}, u32[]{:S(2)}) collective-permute-start(f32[20,2,16,128]{3,2,1,0:T(8,128)S(1)} %get-tuple-element.17), channel_id=1, source_target_pairs={{4,0},{8,4},{12,8},{5,1},{9,5},{13,9},{6,2},{10,6},{14,10},{7,3},{... | collective-permute-start | bytes 983048 | tf_op jit(solution)/shard_map/ppermute | solution.py:20
  274.8 2.8 collective-permute-done.44
  283.2 4.9 %collective-permute-start.47 = (f32[20,20,2,128]{3,2,1,0:T(2,128)}, f32[20,20,2,128]{3,2,1,0:T(2,128)}, u32[]{:S(2)}, u32[]{:S(2)}) collective-permute-start(f32[20,20,2,128]{3,2,1,0:T(2,128)} %get-tuple-element.12), channel_id=1, source_target_pairs={{1,0},{2,1},{3,2},{5,4},{6,5},{7,6},{9,8},{10,9},{11,10},{13,12},{... | collective-permute-start | bytes 1228808 | tf_op jit(solution)/shard_map/ppermute | solution.py:20
  288.1 2.8 reshape_reshape.3
  293.6 4.6 %fusion.11 = f32[20,20,20,128]{3,2,1,0:T(8,128)S(1)} fusion(f32[16,16,16,64]{3,2,1,0:T(8,128)S(1)} %reshape.351, f32[20,20,2,128]{3,2,1,0:T(2,128)} %collective-permute-done.47, f32[20,2,16,128]{3,2,1,0:T(8,128)S(1)} %collective-permute-done.45, f32[2,16,16,128]{3,2,1,0:T(8,128)S(1)} %collective-permute-done.43, f32[16,16,16,64]{3,2,1,0:T(8,128)} %copy-done.4, ...), kind=kLoop, calls=%fused_computation.13 | loop fusion | flops 7168000 | bytes 8192000 | tf_op jit(solution)/shard_map/concatenate | solution.py:21
  298.2 9.5 %fusion.35 = f32[18,18,18,64]{3,2,1,0:T(8,128)S(1)} fusion(f32[16,16,16,64]{3,2,1,0:T(8,128)S(1)} %reshape.351, f32[20,20,2,128]{3,2,1,0:T(2,128)} %collective-permute-done.46, f32[20,2,16,128]{3,2,1,0:T(8,128)S(1)} %collective-permute-done.45, f32[20,2,16,128]{3,2,1,0:T(8,128)S(1)} %collective-permute-done.44, ...), kind=kLoop, calls=%fused_computation.41 | loop fusion | flops 8584704 | bytes 14570272 | tf_op jit(solution)/shard_map/mul | solution.py:108
  307.7 3.1 fusion.61
  310.8 2.9 reshape.365
  313.7 5.2 %convolution_bitcast_fusion = f32[64,64]{0,1:T(8,128)S(1)} fusion(f32[4096,64]{1,0:T(8,128)S(1)} %bitcast.73, f32[4096,64]{1,0:T(8,128)} %reshape_reshape.3), kind=kOutput, calls=%fused_computation.108 | convolution fusion | flops 201326592 | bytes 2113536 | tf_op jit(solution)/shard_map/dot_general | solution.py:131
  318.9 43.0 %psum.7 = f32[64,64]{0,1:T(8,128)S(1)} all-reduce(f32[64,64]{0,1:T(8,128)S(1)} %convolution_bitcast_fusion), channel_id=1, replica_groups=mesh['gx'=2,'gy'=4,'gz'=4] {'gx','gy','gz'}, use_global_device_ids=true, to_apply=%region_6.7 | all-reduce | flops 4096 | bytes 32768 | tf_op jit(solution)/shard_map/psum | solution.py:137
  (211 shorter events, 98.7 us)
Async XLA Ops:
  4.8 9.9 %collective-permute-start = (f32[2,16,16,128]{3,2,1,0:T(8,128)S(1)}, f32[2,16,16,128]{3,2,1,0:T(8,128)S(1)}, u32[]{:S(2)}, u32[]{:S(2)}) collective-permute-start(f32[2,16,16,128]{3,2,1,0:T(8,128)S(1)} %get-tuple-element.22), channel_id=1, source_target_pairs={{0,16},{1,17},{2,18},{3,19},{4,20},{5,21},{6,22},{7,23},{8,24},{9,... | collective-permute-start | bytes 786440 | tf_op jit(solution)/shard_map/ppermute | solution.py:19
  6.1 9.8 %collective-permute-start.1 = (f32[2,16,16,128]{3,2,1,0:T(8,128)S(1)}, f32[2,16,16,128]{3,2,1,0:T(8,128)S(1)}, u32[]{:S(2)}, u32[]{:S(2)}) collective-permute-start(f32[2,16,16,128]{3,2,1,0:T(8,128)S(1)} %get-tuple-element.10), channel_id=1, source_target_pairs={{16,0},{17,1},{18,2},{19,3},{20,4},{21,5},{22,6},{23,7},{24,8},{25... | collective-permute-start | bytes 786440 | tf_op jit(solution)/shard_map/ppermute | solution.py:20
  18.2 8.4 %collective-permute-start.2 = (f32[20,2,16,128]{3,2,1,0:T(8,128)S(1)}, f32[20,2,16,128]{3,2,1,0:T(8,128)S(1)}, u32[]{:S(2)}, u32[]{:S(2)}) collective-permute-start(f32[20,2,16,128]{3,2,1,0:T(8,128)S(1)} %get-tuple-element.18), channel_id=1, source_target_pairs={{0,4},{4,8},{8,12},{1,5},{5,9},{9,13},{2,6},{6,10},{10,14},{3,7},{... | collective-permute-start | bytes 983048 | tf_op jit(solution)/shard_map/ppermute | solution.py:19
  20.1 8.2 %collective-permute-start.3 = (f32[20,2,16,128]{3,2,1,0:T(8,128)S(1)}, f32[20,2,16,128]{3,2,1,0:T(8,128)S(1)}, u32[]{:S(2)}, u32[]{:S(2)}) collective-permute-start(f32[20,2,16,128]{3,2,1,0:T(8,128)S(1)} %get-tuple-element.19), channel_id=1, source_target_pairs={{4,0},{8,4},{12,8},{5,1},{9,5},{13,9},{6,2},{10,6},{14,10},{7,3},{... | collective-permute-start | bytes 983048 | tf_op jit(solution)/shard_map/ppermute | solution.py:20
  29.3 9.8 %collective-permute-start.4 = (f32[20,20,2,128]{3,2,1,0:T(2,128)S(1)}, f32[20,20,2,128]{3,2,1,0:T(2,128)S(1)}, u32[]{:S(2)}, u32[]{:S(2)}) collective-permute-start(f32[20,20,2,128]{3,2,1,0:T(2,128)S(1)} %get-tuple-element.15), channel_id=1, source_target_pairs={{0,1},{1,2},{2,3},{4,5},{5,6},{6,7},{8,9},{9,10},{10,11},{12,13},{... | collective-permute-start | bytes 1228808 | tf_op jit(solution)/shard_map/ppermute | solution.py:19
  32.8 9.8 %collective-permute-start.5 = (f32[20,20,2,128]{3,2,1,0:T(2,128)S(1)}, f32[20,20,2,128]{3,2,1,0:T(2,128)S(1)}, u32[]{:S(2)}, u32[]{:S(2)}) collective-permute-start(f32[20,20,2,128]{3,2,1,0:T(2,128)S(1)} %get-tuple-element.14), channel_id=1, source_target_pairs={{1,0},{2,1},{3,2},{5,4},{6,5},{7,6},{9,8},{10,9},{11,10},{13,12},{... | collective-permute-start | bytes 1228808 | tf_op jit(solution)/shard_map/ppermute | solution.py:20
  60.9 6.6 %collective-permute-start.6 = (f32[2,8,8,128]{3,2,1,0:T(8,128)S(1)}, f32[2,8,8,128]{3,2,1,0:T(8,128)S(1)}, u32[]{:S(2)}, u32[]{:S(2)}) collective-permute-start(f32[2,8,8,128]{3,2,1,0:T(8,128)S(1)} %get-tuple-element.33), channel_id=1, source_target_pairs={{0,16},{1,17},{2,18},{3,19},{4,20},{5,21},{6,22},{7,23},{8,24},{9,... | collective-permute-start | bytes 196616 | tf_op jit(solution)/shard_map/ppermute | solution.py:19
  62.2 6.4 %collective-permute-start.7 = (f32[2,8,8,128]{3,2,1,0:T(8,128)S(1)}, f32[2,8,8,128]{3,2,1,0:T(8,128)S(1)}, u32[]{:S(2)}, u32[]{:S(2)}) collective-permute-start(f32[2,8,8,128]{3,2,1,0:T(8,128)S(1)} %get-tuple-element.8), channel_id=1, source_target_pairs={{16,0},{17,1},{18,2},{19,3},{20,4},{21,5},{22,6},{23,7},{24,8},{25... | collective-permute-start | bytes 196616 | tf_op jit(solution)/shard_map/ppermute | solution.py:20
  68.8 5.9 %collective-permute-start.8 = (f32[12,2,8,128]{3,2,1,0:T(8,128)S(1)}, f32[12,2,8,128]{3,2,1,0:T(8,128)S(1)}, u32[]{:S(2)}, u32[]{:S(2)}) collective-permute-start(f32[12,2,8,128]{3,2,1,0:T(8,128)S(1)} %get-tuple-element.29), channel_id=1, source_target_pairs={{0,4},{4,8},{8,12},{1,5},{5,9},{9,13},{2,6},{6,10},{10,14},{3,7},{... | collective-permute-start | bytes 294920 | tf_op jit(solution)/shard_map/ppermute | solution.py:19
  70.7 5.8 %collective-permute-start.9 = (f32[12,2,8,128]{3,2,1,0:T(8,128)S(1)}, f32[12,2,8,128]{3,2,1,0:T(8,128)S(1)}, u32[]{:S(2)}, u32[]{:S(2)}) collective-permute-start(f32[12,2,8,128]{3,2,1,0:T(8,128)S(1)} %get-tuple-element.30), channel_id=1, source_target_pairs={{4,0},{8,4},{12,8},{5,1},{9,5},{13,9},{6,2},{10,6},{14,10},{7,3},{... | collective-permute-start | bytes 294920 | tf_op jit(solution)/shard_map/ppermute | solution.py:20
  76.8 7.0 %collective-permute-start.10 = (f32[12,12,2,128]{3,2,1,0:T(2,128)S(1)}, f32[12,12,2,128]{3,2,1,0:T(2,128)S(1)}, u32[]{:S(2)}, u32[]{:S(2)}) collective-permute-start(f32[12,12,2,128]{3,2,1,0:T(2,128)S(1)} %get-tuple-element.26), channel_id=1, source_target_pairs={{0,1},{1,2},{2,3},{4,5},{5,6},{6,7},{8,9},{9,10},{10,11},{12,13},{... | collective-permute-start | bytes 442376 | tf_op jit(solution)/shard_map/ppermute | solution.py:19
  80.3 7.0 %collective-permute-start.11 = (f32[12,12,2,128]{3,2,1,0:T(2,128)S(1)}, f32[12,12,2,128]{3,2,1,0:T(2,128)S(1)}, u32[]{:S(2)}, u32[]{:S(2)}) collective-permute-start(f32[12,12,2,128]{3,2,1,0:T(2,128)S(1)} %get-tuple-element.25), channel_id=1, source_target_pairs={{1,0},{2,1},{3,2},{5,4},{6,5},{7,6},{9,8},{10,9},{11,10},{13,12},{... | collective-permute-start | bytes 442376 | tf_op jit(solution)/shard_map/ppermute | solution.py:20
  89.9 6.1 %collective-permute-start.12 = (f32[2,4,4,128]{3,2,1,0:T(4,128)S(1)}, f32[2,4,4,128]{3,2,1,0:T(4,128)S(1)}, u32[]{:S(2)}, u32[]{:S(2)}) collective-permute-start(f32[2,4,4,128]{3,2,1,0:T(4,128)S(1)} %get-tuple-element.46), channel_id=1, source_target_pairs={{0,16},{1,17},{2,18},{3,19},{4,20},{5,21},{6,22},{7,23},{8,24},{9,... | collective-permute-start | bytes 49160 | tf_op jit(solution)/shard_map/ppermute | solution.py:19
  91.2 6.0 %collective-permute-start.13 = (f32[2,4,4,128]{3,2,1,0:T(4,128)S(1)}, f32[2,4,4,128]{3,2,1,0:T(4,128)S(1)}, u32[]{:S(2)}, u32[]{:S(2)}) collective-permute-start(f32[2,4,4,128]{3,2,1,0:T(4,128)S(1)} %get-tuple-element.47), channel_id=1, source_target_pairs={{16,0},{17,1},{18,2},{19,3},{20,4},{21,5},{22,6},{23,7},{24,8},{25... | collective-permute-start | bytes 49160 | tf_op jit(solution)/shard_map/ppermute | solution.py:20
  97.2 5.7 %collective-permute-start.14 = (f32[8,2,4,128]{3,2,1,0:T(4,128)S(1)}, f32[8,2,4,128]{3,2,1,0:T(4,128)S(1)}, u32[]{:S(2)}, u32[]{:S(2)}) collective-permute-start(f32[8,2,4,128]{3,2,1,0:T(4,128)S(1)} %get-tuple-element.44), channel_id=1, source_target_pairs={{0,4},{4,8},{8,12},{1,5},{5,9},{9,13},{2,6},{6,10},{10,14},{3,7},{... | collective-permute-start | bytes 98312 | tf_op jit(solution)/shard_map/ppermute | solution.py:19
  99.2 5.2 %collective-permute-start.15 = (f32[8,2,4,128]{3,2,1,0:T(4,128)S(1)}, f32[8,2,4,128]{3,2,1,0:T(4,128)S(1)}, u32[]{:S(2)}, u32[]{:S(2)}) collective-permute-start(f32[8,2,4,128]{3,2,1,0:T(4,128)S(1)} %get-tuple-element.45), channel_id=1, source_target_pairs={{4,0},{8,4},{12,8},{5,1},{9,5},{13,9},{6,2},{10,6},{14,10},{7,3},{... | collective-permute-start | bytes 98312 | tf_op jit(solution)/shard_map/ppermute | solution.py:20
  104.6 6.4 %collective-permute-start.16 = (f32[8,8,2,128]{3,2,1,0:T(2,128)S(1)}, f32[8,8,2,128]{3,2,1,0:T(2,128)S(1)}, u32[]{:S(2)}, u32[]{:S(2)}) collective-permute-start(f32[8,8,2,128]{3,2,1,0:T(2,128)S(1)} %get-tuple-element.39), channel_id=1, source_target_pairs={{0,1},{1,2},{2,3},{4,5},{5,6},{6,7},{8,9},{9,10},{10,11},{12,13},{... | collective-permute-start | bytes 196616 | tf_op jit(solution)/shard_map/ppermute | solution.py:19
  106.5 6.2 %collective-permute-start.17 = (f32[8,8,2,128]{3,2,1,0:T(2,128)S(1)}, f32[8,8,2,128]{3,2,1,0:T(2,128)S(1)}, u32[]{:S(2)}, u32[]{:S(2)}) collective-permute-start(f32[8,8,2,128]{3,2,1,0:T(2,128)S(1)} %get-tuple-element.38), channel_id=1, source_target_pairs={{1,0},{2,1},{3,2},{5,4},{6,5},{7,6},{9,8},{10,9},{11,10},{13,12},{... | collective-permute-start | bytes 196616 | tf_op jit(solution)/shard_map/ppermute | solution.py:20
  113.1 6.6 %collective-permute-start.18 = (f32[2,2,2,128]{3,2,1,0:T(2,128)S(1)}, f32[2,2,2,128]{3,2,1,0:T(2,128)S(1)}, u32[]{:S(2)}, u32[]{:S(2)}) collective-permute-start(f32[2,2,2,128]{3,2,1,0:T(2,128)S(1)} %pad_maximum_fusion.46), channel_id=1, source_target_pairs={{0,16},{1,17},{2,18},{3,19},{4,20},{5,21},{6,22},{7,23},{8,24},{9,... | collective-permute-start | bytes 12296 | tf_op jit(solution)/shard_map/ppermute | solution.py:19
  114.4 5.9 %collective-permute-start.19 = (f32[2,2,2,128]{3,2,1,0:T(2,128)S(1)}, f32[2,2,2,128]{3,2,1,0:T(2,128)S(1)}, u32[]{:S(2)}, u32[]{:S(2)}) collective-permute-start(f32[2,2,2,128]{3,2,1,0:T(2,128)S(1)} %pad_maximum_fusion.46), channel_id=1, source_target_pairs={{16,0},{17,1},{18,2},{19,3},{20,4},{21,5},{22,6},{23,7},{24,8},{25... | collective-permute-start | bytes 12296 | tf_op jit(solution)/shard_map/ppermute | solution.py:20
  120.3 5.6 %collective-permute-start.20 = (f32[6,2,2,128]{3,2,1,0:T(2,128)S(1)}, f32[6,2,2,128]{3,2,1,0:T(2,128)S(1)}, u32[]{:S(2)}, u32[]{:S(2)}) collective-permute-start(f32[6,2,2,128]{3,2,1,0:T(2,128)S(1)} %fusion.281), channel_id=1, source_target_pairs={{0,4},{4,8},{8,12},{1,5},{5,9},{9,13},{2,6},{6,10},{10,14},{3,7},{... | collective-permute-start | bytes 36872 | tf_op jit(solution)/shard_map/ppermute | solution.py:19
  122.3 5.0 %collective-permute-start.21 = (f32[6,2,2,128]{3,2,1,0:T(2,128)S(1)}, f32[6,2,2,128]{3,2,1,0:T(2,128)S(1)}, u32[]{:S(2)}, u32[]{:S(2)}) collective-permute-start(f32[6,2,2,128]{3,2,1,0:T(2,128)S(1)} %fusion.281), channel_id=1, source_target_pairs={{4,0},{8,4},{12,8},{5,1},{9,5},{13,9},{6,2},{10,6},{14,10},{7,3},{... | collective-permute-start | bytes 36872 | tf_op jit(solution)/shard_map/ppermute | solution.py:20
  128.0 6.0 %collective-permute-start.22 = (f32[6,6,2,128]{3,2,1,0:T(2,128)}, f32[6,6,2,128]{3,2,1,0:T(2,128)S(1)}, u32[]{:S(2)}, u32[]{:S(2)}) collective-permute-start(f32[6,6,2,128]{3,2,1,0:T(2,128)} %fusion.211), channel_id=1, source_target_pairs={{0,1},{1,2},{2,3},{4,5},{5,6},{6,7},{8,9},{9,10},{10,11},{12,13},{... | collective-permute-start | bytes 110600 | tf_op jit(solution)/shard_map/ppermute | solution.py:19
  129.9 6.2 %collective-permute-start.23 = (f32[6,6,2,128]{3,2,1,0:T(2,128)}, f32[6,6,2,128]{3,2,1,0:T(2,128)}, u32[]{:S(2)}, u32[]{:S(2)}) collective-permute-start(f32[6,6,2,128]{3,2,1,0:T(2,128)} %fusion.211), channel_id=1, source_target_pairs={{1,0},{2,1},{3,2},{5,4},{6,5},{7,6},{9,8},{10,9},{11,10},{13,12},{... | collective-permute-start | bytes 110600 | tf_op jit(solution)/shard_map/ppermute | solution.py:20
  182.0 5.8 %collective-permute-start.24 = (f32[2,2,2,128]{3,2,1,0:T(2,128)S(1)}, f32[2,2,2,128]{3,2,1,0:T(2,128)S(1)}, u32[]{:S(2)}, u32[]{:S(2)}) collective-permute-start(f32[2,2,2,128]{3,2,1,0:T(2,128)S(1)} %pad_maximum_fusion.47), channel_id=1, source_target_pairs={{0,16},{1,17},{2,18},{3,19},{4,20},{5,21},{6,22},{7,23},{8,24},{9,... | collective-permute-start | bytes 12296 | tf_op jit(solution)/shard_map/ppermute | solution.py:19
  183.3 5.9 %collective-permute-start.25 = (f32[2,2,2,128]{3,2,1,0:T(2,128)S(1)}, f32[2,2,2,128]{3,2,1,0:T(2,128)S(1)}, u32[]{:S(2)}, u32[]{:S(2)}) collective-permute-start(f32[2,2,2,128]{3,2,1,0:T(2,128)S(1)} %pad_maximum_fusion.47), channel_id=1, source_target_pairs={{16,0},{17,1},{18,2},{19,3},{20,4},{21,5},{22,6},{23,7},{24,8},{25... | collective-permute-start | bytes 12296 | tf_op jit(solution)/shard_map/ppermute | solution.py:20
  189.3 5.6 %collective-permute-start.26 = (f32[6,2,2,128]{3,2,1,0:T(2,128)S(1)}, f32[6,2,2,128]{3,2,1,0:T(2,128)S(1)}, u32[]{:S(2)}, u32[]{:S(2)}) collective-permute-start(f32[6,2,2,128]{3,2,1,0:T(2,128)S(1)} %fusion.283), channel_id=1, source_target_pairs={{0,4},{4,8},{8,12},{1,5},{5,9},{9,13},{2,6},{6,10},{10,14},{3,7},{... | collective-permute-start | bytes 36872 | tf_op jit(solution)/shard_map/ppermute | solution.py:19
  191.2 5.0 %collective-permute-start.27 = (f32[6,2,2,128]{3,2,1,0:T(2,128)S(1)}, f32[6,2,2,128]{3,2,1,0:T(2,128)S(1)}, u32[]{:S(2)}, u32[]{:S(2)}) collective-permute-start(f32[6,2,2,128]{3,2,1,0:T(2,128)S(1)} %fusion.283), channel_id=1, source_target_pairs={{4,0},{8,4},{12,8},{5,1},{9,5},{13,9},{6,2},{10,6},{14,10},{7,3},{... | collective-permute-start | bytes 36872 | tf_op jit(solution)/shard_map/ppermute | solution.py:20
  196.3 5.8 %collective-permute-start.28 = (f32[6,6,2,128]{3,2,1,0:T(2,128)S(1)}, f32[6,6,2,128]{3,2,1,0:T(2,128)S(1)}, u32[]{:S(2)}, u32[]{:S(2)}) collective-permute-start(f32[6,6,2,128]{3,2,1,0:T(2,128)S(1)} %fusion.215), channel_id=1, source_target_pairs={{0,1},{1,2},{2,3},{4,5},{5,6},{6,7},{8,9},{9,10},{10,11},{12,13},{... | collective-permute-start | bytes 110600 | tf_op jit(solution)/shard_map/ppermute | solution.py:19
  198.8 5.9 %collective-permute-start.29 = (f32[6,6,2,128]{3,2,1,0:T(2,128)S(1)}, f32[6,6,2,128]{3,2,1,0:T(2,128)S(1)}, u32[]{:S(2)}, u32[]{:S(2)}) collective-permute-start(f32[6,6,2,128]{3,2,1,0:T(2,128)S(1)} %fusion.215), channel_id=1, source_target_pairs={{1,0},{2,1},{3,2},{5,4},{6,5},{7,6},{9,8},{10,9},{11,10},{13,12},{... | collective-permute-start | bytes 110600 | tf_op jit(solution)/shard_map/ppermute | solution.py:20
  205.1 5.9 %collective-permute-start.30 = (f32[2,4,4,128]{3,2,1,0:T(4,128)S(1)}, f32[2,4,4,128]{3,2,1,0:T(4,128)S(1)}, u32[]{:S(2)}, u32[]{:S(2)}) collective-permute-start(f32[2,4,4,128]{3,2,1,0:T(4,128)S(1)} %get-tuple-element.42), channel_id=1, source_target_pairs={{0,16},{1,17},{2,18},{3,19},{4,20},{5,21},{6,22},{7,23},{8,24},{9,... | collective-permute-start | bytes 49160 | tf_op jit(solution)/shard_map/ppermute | solution.py:19
  206.4 6.0 %collective-permute-start.31 = (f32[2,4,4,128]{3,2,1,0:T(4,128)S(1)}, f32[2,4,4,128]{3,2,1,0:T(4,128)S(1)}, u32[]{:S(2)}, u32[]{:S(2)}) collective-permute-start(f32[2,4,4,128]{3,2,1,0:T(4,128)S(1)} %get-tuple-element.43), channel_id=1, source_target_pairs={{16,0},{17,1},{18,2},{19,3},{20,4},{21,5},{22,6},{23,7},{24,8},{25... | collective-permute-start | bytes 49160 | tf_op jit(solution)/shard_map/ppermute | solution.py:20
  212.5 5.6 %collective-permute-start.32 = (f32[8,2,4,128]{3,2,1,0:T(4,128)S(1)}, f32[8,2,4,128]{3,2,1,0:T(4,128)S(1)}, u32[]{:S(2)}, u32[]{:S(2)}) collective-permute-start(f32[8,2,4,128]{3,2,1,0:T(4,128)S(1)} %get-tuple-element.40), channel_id=1, source_target_pairs={{0,4},{4,8},{8,12},{1,5},{5,9},{9,13},{2,6},{6,10},{10,14},{3,7},{... | collective-permute-start | bytes 98312 | tf_op jit(solution)/shard_map/ppermute | solution.py:19
  214.4 5.2 %collective-permute-start.33 = (f32[8,2,4,128]{3,2,1,0:T(4,128)S(1)}, f32[8,2,4,128]{3,2,1,0:T(4,128)S(1)}, u32[]{:S(2)}, u32[]{:S(2)}) collective-permute-start(f32[8,2,4,128]{3,2,1,0:T(4,128)S(1)} %get-tuple-element.41), channel_id=1, source_target_pairs={{4,0},{8,4},{12,8},{5,1},{9,5},{13,9},{6,2},{10,6},{14,10},{7,3},{... | collective-permute-start | bytes 98312 | tf_op jit(solution)/shard_map/ppermute | solution.py:20
  219.8 6.2 %collective-permute-start.34 = (f32[8,8,2,128]{3,2,1,0:T(2,128)S(1)}, f32[8,8,2,128]{3,2,1,0:T(2,128)S(1)}, u32[]{:S(2)}, u32[]{:S(2)}) collective-permute-start(f32[8,8,2,128]{3,2,1,0:T(2,128)S(1)} %get-tuple-element.37), channel_id=1, source_target_pairs={{0,1},{1,2},{2,3},{4,5},{5,6},{6,7},{8,9},{9,10},{10,11},{12,13},{... | collective-permute-start | bytes 196616 | tf_op jit(solution)/shard_map/ppermute | solution.py:19
  221.7 6.2 %collective-permute-start.35 = (f32[8,8,2,128]{3,2,1,0:T(2,128)S(1)}, f32[8,8,2,128]{3,2,1,0:T(2,128)S(1)}, u32[]{:S(2)}, u32[]{:S(2)}) collective-permute-start(f32[8,8,2,128]{3,2,1,0:T(2,128)S(1)} %get-tuple-element.36), channel_id=1, source_target_pairs={{1,0},{2,1},{3,2},{5,4},{6,5},{7,6},{9,8},{10,9},{11,10},{13,12},{... | collective-permute-start | bytes 196616 | tf_op jit(solution)/shard_map/ppermute | solution.py:20
  229.3 6.2 %collective-permute-start.36 = (f32[2,8,8,128]{3,2,1,0:T(8,128)S(1)}, f32[2,8,8,128]{3,2,1,0:T(8,128)S(1)}, u32[]{:S(2)}, u32[]{:S(2)}) collective-permute-start(f32[2,8,8,128]{3,2,1,0:T(8,128)S(1)} %get-tuple-element.31), channel_id=1, source_target_pairs={{0,16},{1,17},{2,18},{3,19},{4,20},{5,21},{6,22},{7,23},{8,24},{9,... | collective-permute-start | bytes 196616 | tf_op jit(solution)/shard_map/ppermute | solution.py:19
  230.5 6.4 %collective-permute-start.37 = (f32[2,8,8,128]{3,2,1,0:T(8,128)S(1)}, f32[2,8,8,128]{3,2,1,0:T(8,128)S(1)}, u32[]{:S(2)}, u32[]{:S(2)}) collective-permute-start(f32[2,8,8,128]{3,2,1,0:T(8,128)S(1)} %get-tuple-element.32), channel_id=1, source_target_pairs={{16,0},{17,1},{18,2},{19,3},{20,4},{21,5},{22,6},{23,7},{24,8},{25... | collective-permute-start | bytes 196616 | tf_op jit(solution)/shard_map/ppermute | solution.py:20
  237.2 5.9 %collective-permute-start.38 = (f32[12,2,8,128]{3,2,1,0:T(8,128)S(1)}, f32[12,2,8,128]{3,2,1,0:T(8,128)S(1)}, u32[]{:S(2)}, u32[]{:S(2)}) collective-permute-start(f32[12,2,8,128]{3,2,1,0:T(8,128)S(1)} %get-tuple-element.27), channel_id=1, source_target_pairs={{0,4},{4,8},{8,12},{1,5},{5,9},{9,13},{2,6},{6,10},{10,14},{3,7},{... | collective-permute-start | bytes 294920 | tf_op jit(solution)/shard_map/ppermute | solution.py:19
  239.1 5.8 %collective-permute-start.39 = (f32[12,2,8,128]{3,2,1,0:T(8,128)S(1)}, f32[12,2,8,128]{3,2,1,0:T(8,128)S(1)}, u32[]{:S(2)}, u32[]{:S(2)}) collective-permute-start(f32[12,2,8,128]{3,2,1,0:T(8,128)S(1)} %get-tuple-element.28), channel_id=1, source_target_pairs={{4,0},{8,4},{12,8},{5,1},{9,5},{13,9},{6,2},{10,6},{14,10},{7,3},{... | collective-permute-start | bytes 294920 | tf_op jit(solution)/shard_map/ppermute | solution.py:20
  245.2 7.0 %collective-permute-start.40 = (f32[12,12,2,128]{3,2,1,0:T(2,128)S(1)}, f32[12,12,2,128]{3,2,1,0:T(2,128)S(1)}, u32[]{:S(2)}, u32[]{:S(2)}) collective-permute-start(f32[12,12,2,128]{3,2,1,0:T(2,128)S(1)} %get-tuple-element.24), channel_id=1, source_target_pairs={{0,1},{1,2},{2,3},{4,5},{5,6},{6,7},{8,9},{9,10},{10,11},{12,13},{... | collective-permute-start | bytes 442376 | tf_op jit(solution)/shard_map/ppermute | solution.py:19
  247.1 7.0 %collective-permute-start.41 = (f32[12,12,2,128]{3,2,1,0:T(2,128)S(1)}, f32[12,12,2,128]{3,2,1,0:T(2,128)S(1)}, u32[]{:S(2)}, u32[]{:S(2)}) collective-permute-start(f32[12,12,2,128]{3,2,1,0:T(2,128)S(1)} %get-tuple-element.23), channel_id=1, source_target_pairs={{1,0},{2,1},{3,2},{5,4},{6,5},{7,6},{9,8},{10,9},{11,10},{13,12},{... | collective-permute-start | bytes 442376 | tf_op jit(solution)/shard_map/ppermute | solution.py:20
  258.8 8.3 %collective-permute-start.42 = (f32[2,16,16,128]{3,2,1,0:T(8,128)S(1)}, f32[2,16,16,128]{3,2,1,0:T(8,128)S(1)}, u32[]{:S(2)}, u32[]{:S(2)}) collective-permute-start(f32[2,16,16,128]{3,2,1,0:T(8,128)S(1)} %get-tuple-element.20), channel_id=1, source_target_pairs={{0,16},{1,17},{2,18},{3,19},{4,20},{5,21},{6,22},{7,23},{8,24},{9,... | collective-permute-start | bytes 786440 | tf_op jit(solution)/shard_map/ppermute | solution.py:19
  260.1 8.4 %collective-permute-start.43 = (f32[2,16,16,128]{3,2,1,0:T(8,128)S(1)}, f32[2,16,16,128]{3,2,1,0:T(8,128)S(1)}, u32[]{:S(2)}, u32[]{:S(2)}) collective-permute-start(f32[2,16,16,128]{3,2,1,0:T(8,128)S(1)} %get-tuple-element.21), channel_id=1, source_target_pairs={{16,0},{17,1},{18,2},{19,3},{20,4},{21,5},{22,6},{23,7},{24,8},{25... | collective-permute-start | bytes 786440 | tf_op jit(solution)/shard_map/ppermute | solution.py:20
  269.3 8.4 %collective-permute-start.44 = (f32[20,2,16,128]{3,2,1,0:T(8,128)S(1)}, f32[20,2,16,128]{3,2,1,0:T(8,128)S(1)}, u32[]{:S(2)}, u32[]{:S(2)}) collective-permute-start(f32[20,2,16,128]{3,2,1,0:T(8,128)S(1)} %get-tuple-element.16), channel_id=1, source_target_pairs={{0,4},{4,8},{8,12},{1,5},{5,9},{9,13},{2,6},{6,10},{10,14},{3,7},{... | collective-permute-start | bytes 983048 | tf_op jit(solution)/shard_map/ppermute | solution.py:19
  271.2 8.2 %collective-permute-start.45 = (f32[20,2,16,128]{3,2,1,0:T(8,128)S(1)}, f32[20,2,16,128]{3,2,1,0:T(8,128)S(1)}, u32[]{:S(2)}, u32[]{:S(2)}) collective-permute-start(f32[20,2,16,128]{3,2,1,0:T(8,128)S(1)} %get-tuple-element.17), channel_id=1, source_target_pairs={{4,0},{8,4},{12,8},{5,1},{9,5},{13,9},{6,2},{10,6},{14,10},{7,3},{... | collective-permute-start | bytes 983048 | tf_op jit(solution)/shard_map/ppermute | solution.py:20
  281.3 10.2 %collective-permute-start.46 = (f32[20,20,2,128]{3,2,1,0:T(2,128)}, f32[20,20,2,128]{3,2,1,0:T(2,128)}, u32[]{:S(2)}, u32[]{:S(2)}) collective-permute-start(f32[20,20,2,128]{3,2,1,0:T(2,128)} %get-tuple-element.13), channel_id=1, source_target_pairs={{0,1},{1,2},{2,3},{4,5},{5,6},{6,7},{8,9},{9,10},{10,11},{12,13},{... | collective-permute-start | bytes 1228808 | tf_op jit(solution)/shard_map/ppermute | solution.py:19
  283.2 10.5 %collective-permute-start.47 = (f32[20,20,2,128]{3,2,1,0:T(2,128)}, f32[20,20,2,128]{3,2,1,0:T(2,128)}, u32[]{:S(2)}, u32[]{:S(2)}) collective-permute-start(f32[20,20,2,128]{3,2,1,0:T(2,128)} %get-tuple-element.12), channel_id=1, source_target_pairs={{1,0},{2,1},{3,2},{5,4},{6,5},{7,6},{9,8},{10,9},{11,10},{13,12},{... | collective-permute-start | bytes 1228808 | tf_op jit(solution)/shard_map/ppermute | solution.py:20
  (19 other events, 295.5 us)
where the time goes:
time: 365 us; the launch traced here: 363 us
  starting transfers between devices  139 us (38%)
  blocking collectives  85.3 us (23%)
  waiting for transfers between devices  62.1 us (17%)
  other arithmetic  54.9 us (15%)
  local copies, waits for them, and re-layouts  14.3 us (4%)
  matrix products  5.15 us (1%)
    ppermute x24, starting transfers between devices, extended_2(): after = lax.ppermute(initial, axis, down)  94.3 us
    ppermute x24, starting transfers between devices, extended_2(): before = lax.ppermute(last, axis, up)  44.7 us
    psum x1, blocking collectives, local(): summed = lax.psum(partial_block, ('gx', 'gy', 'gz'))  43 us
    unnamed x1, blocking collectives  42.3 us
    ppermute x24, waiting for transfers between devices, extended_2(): after = lax.ppermute(initial, axis, down)  42.2 us
    mul x8, other arithmetic, double_sweep(): sweep_inner(extended[..., :count], source_wide, factor)  23.4 us
    ppermute x24, waiting for transfers between devices, extended_2(): before = lax.ppermute(last, axis, up)  19.9 us
    concatenate x24, other arithmetic, extended_2(): x = jnp.concatenate([before, x, after], axis=dim)  15.6 us
  transfers between devices with their start and end apart: 48, of which 37 were waited for; matrix products, arithmetic and copies ran while one was open for 1% of the time, Pallas kernels for 0%

commit v1 on v0

--- a/solution.py
+++ b/solution.py
@@ -134,7 +134,7 @@
         precision=lax.Precision.HIGHEST,
         preferred_element_type=jnp.float32,
     )
-    summed = lax.psum(partial_block, ("gx", "gy", "gz"))
+    summed = jnp.sum(lax.all_gather(partial_block, ("gx", "gy", "gz")), axis=0)
     total_cells = (
         cells_x
         * cells_y

time: 365 us -> 397 us (1.088)
  the two profiles are of different devices: /device:TPU:14 before, /device:TPU:0 now
where the time goes in v1:
time: 397 us; the launch traced here: 395 us
  waiting for transfers between devices  117 us (29%)
  blocking collectives  111 us (28%)
  starting transfers between devices  90.3 us (23%)
  other arithmetic  55 us (14%)
  local copies, waits for them, and re-layouts  14.5 us (4%)
  matrix products  5.15 us (1%)
    ppermute x24, waiting for transfers between devices, extended_2(): after = lax.ppermute(initial, axis, down)  98.7 us
    all_gather x1, blocking collectives, local(): summed = jnp.sum(lax.all_gather(partial_block, ('gx', 'gy', 'gz')), axis=0)  72.9 us
    ppermute x24, starting transfers between devices, extended_2(): before = lax.ppermute(last, axis, up)  58.9 us
    unnamed x1, blocking collectives  38.2 us
    ppermute x24, starting transfers between devices, extended_2(): after = lax.ppermute(initial, axis, down)  31.4 us
    mul x8, other arithmetic, double_sweep(): sweep_inner(extended[..., :count], source_wide, factor)  23.4 us
    ppermute x24, waiting for transfers between devices, extended_2(): before = lax.ppermute(last, axis, up)  18.4 us
    concatenate x24, other arithmetic, extended_2(): x = jnp.concatenate([before, x, after], axis=dim)  15.6 us
  transfers between devices with their start and end apart: 48, of which 35 were waited for; matrix products, arithmetic and copies ran while one was open for 1% of the time, Pallas kernels for 0%

profile of v1, /device:TPU:0, one launch (start us, length us, event | category | flops | bytes accessed | tf_op | source)
XLA Modules:
  0.0 394.9 jit_solution(17594652272153710157)
XLA Ops:
  4.8 4.9 %collective-permute-start = (f32[2,16,16,128]{3,2,1,0:T(8,128)S(1)}, f32[2,16,16,128]{3,2,1,0:T(8,128)S(1)}, u32[]{:S(2)}, u32[]{:S(2)}) collective-permute-start(f32[2,16,16,128]{3,2,1,0:T(8,128)S(1)} %get-tuple-element.20), channel_id=1, source_target_pairs={{0,16},{1,17},{2,18},{3,19},{4,20},{5,21},{6,22},{7,23},{8,24},{9,... | collective-permute-start | bytes 786440 | tf_op jit(solution)/shard_map/ppermute | solution.py:19
  11.1 4.2 %collective-permute-done = f32[2,16,16,128]{3,2,1,0:T(8,128)S(1)} collective-permute-done((f32[2,16,16,128]{3,2,1,0:T(8,128)S(1)}, f32[2,16,16,128]{3,2,1,0:T(8,128)S(1)}, u32[]{:S(2)}, u32[]{:S(2)}) %collective-permute-start) | collective-permute-done | bytes 262176 | tf_op jit(solution)/shard_map/ppermute | solution.py:19
  15.2 4.1 %collective-permute-done.1 = f32[2,16,16,128]{3,2,1,0:T(8,128)S(1)} collective-permute-done((f32[2,16,16,128]{3,2,1,0:T(8,128)S(1)}, f32[2,16,16,128]{3,2,1,0:T(8,128)S(1)}, u32[]{:S(2)}, u32[]{:S(2)}) %collective-permute-start.1) | collective-permute-done | bytes 262176 | tf_op jit(solution)/shard_map/ppermute | solution.py:20
  24.3 3.8 collective-permute-done.3
  29.2 3.5 collective-permute-start.4
  34.2 3.9 collective-permute-done.4
  38.1 4.7 %collective-permute-done.5 = f32[20,20,2,128]{3,2,1,0:T(2,128)S(1)} collective-permute-done((f32[20,20,2,128]{3,2,1,0:T(2,128)S(1)}, f32[20,20,2,128]{3,2,1,0:T(2,128)S(1)}, u32[]{:S(2)}, u32[]{:S(2)}) %collective-permute-start.5) | collective-permute-done | bytes 409632 | tf_op jit(solution)/shard_map/ppermute | solution.py:20
  42.8 3.2 fusion.5
  46.0 8.6 %fusion.23 = f32[18,18,18,64]{3,2,1,0:T(8,128)S(1)} fusion(f32[16,16,16,64]{3,2,1,0:T(8,128)S(1)} %reshape.351, f32[20,20,2,128]{3,2,1,0:T(2,128)S(1)} %collective-permute-done.4, f32[20,2,16,128]{3,2,1,0:T(8,128)S(1)} %collective-permute-done.3, f32[20,2,16,128]{3,2,1,0:T(8,128)S(1)} %collective-permute-done.2, ...), kind=kLoop, calls=%fused_computation.29 | loop fusion | flops 8584704 | bytes 14570272 | tf_op jit(solution)/shard_map/mul | solution.py:108
  54.7 2.6 fusion.63
  57.3 3.0 reduce_sum.61
  64.5 4.1 %collective-permute-done.7 = f32[2,8,8,128]{3,2,1,0:T(8,128)S(1)} collective-permute-done((f32[2,8,8,128]{3,2,1,0:T(8,128)S(1)}, f32[2,8,8,128]{3,2,1,0:T(8,128)S(1)}, u32[]{:S(2)}, u32[]{:S(2)}) %collective-permute-start.7) | collective-permute-done | bytes 65568 | tf_op jit(solution)/shard_map/ppermute | solution.py:20
  68.8 4.5 %collective-permute-start.8 = (f32[12,2,8,128]{3,2,1,0:T(8,128)S(1)}, f32[12,2,8,128]{3,2,1,0:T(8,128)S(1)}, u32[]{:S(2)}, u32[]{:S(2)}) collective-permute-start(f32[12,2,8,128]{3,2,1,0:T(8,128)S(1)} %get-tuple-element.27), channel_id=1, source_target_pairs={{0,4},{4,8},{8,12},{1,5},{5,9},{9,13},{2,6},{6,10},{10,14},{3,7},{... | collective-permute-start | bytes 294920 | tf_op jit(solution)/shard_map/ppermute | solution.py:19
  74.7 3.7 collective-permute-done.9
  78.6 3.5 collective-permute-start.10
  84.8 4.4 %collective-permute-done.11 = f32[12,12,2,128]{3,2,1,0:T(2,128)S(1)} collective-permute-done((f32[12,12,2,128]{3,2,1,0:T(2,128)S(1)}, f32[12,12,2,128]{3,2,1,0:T(2,128)S(1)}, u32[]{:S(2)}, u32[]{:S(2)}) %collective-permute-start.11) | collective-permute-done | bytes 147488 | tf_op jit(solution)/shard_map/ppermute | solution.py:20
  94.7 4.1 %collective-permute-done.13 = f32[2,4,4,128]{3,2,1,0:T(4,128)S(1)} collective-permute-done((f32[2,4,4,128]{3,2,1,0:T(4,128)S(1)}, f32[2,4,4,128]{3,2,1,0:T(4,128)S(1)}, u32[]{:S(2)}, u32[]{:S(2)}) %collective-permute-start.13) | collective-permute-done | bytes 16416 | tf_op jit(solution)/shard_map/ppermute | solution.py:20
  102.6 4.0 %collective-permute-done.15 = f32[8,2,4,128]{3,2,1,0:T(4,128)S(1)} collective-permute-done((f32[8,2,4,128]{3,2,1,0:T(4,128)S(1)}, f32[8,2,4,128]{3,2,1,0:T(4,128)S(1)}, u32[]{:S(2)}, u32[]{:S(2)}) %collective-permute-start.15) | collective-permute-done | bytes 32800 | tf_op jit(solution)/shard_map/ppermute | solution.py:20
  106.8 3.5 collective-permute-start.16
  112.2 4.3 %collective-permute-done.17 = f32[8,8,2,128]{3,2,1,0:T(2,128)S(1)} collective-permute-done((f32[8,8,2,128]{3,2,1,0:T(2,128)S(1)}, f32[8,8,2,128]{3,2,1,0:T(2,128)S(1)}, u32[]{:S(2)}, u32[]{:S(2)}) %collective-permute-start.17) | collective-permute-done | bytes 65568 | tf_op jit(solution)/shard_map/ppermute | solution.py:20
  120.6 3.5 collective-permute-done.19
  127.1 4.1 %collective-permute-done.21 = f32[6,2,2,128]{3,2,1,0:T(2,128)S(1)} collective-permute-done((f32[6,2,2,128]{3,2,1,0:T(2,128)S(1)}, f32[6,2,2,128]{3,2,1,0:T(2,128)S(1)}, u32[]{:S(2)}, u32[]{:S(2)}) %collective-permute-start.21) | collective-permute-done | bytes 12320 | tf_op jit(solution)/shard_map/ppermute | solution.py:20
  135.8 4.2 %collective-permute-done.23 = f32[6,6,2,128]{3,2,1,0:T(2,128)} collective-permute-done((f32[6,6,2,128]{3,2,1,0:T(2,128)}, f32[6,6,2,128]{3,2,1,0:T(2,128)}, u32[]{:S(2)}, u32[]{:S(2)}) %collective-permute-start.23) | collective-permute-done | bytes 36896 | tf_op jit(solution)/shard_map/ppermute | solution.py:20
  142.5 38.2 %all-reduce.11 = f32[2048]{0:T(1024)S(1)} all-reduce(f32[2048]{0:T(1024)S(1)} %multiply_dynamic-update-slice_fusion), channel_id=2, replica_groups=mesh['gx'=2,'gy'=4,'gz'=4] {'gx','gy','gz'}, use_global_device_ids=true, to_apply=%add.11 | all-reduce | flops 2048 | bytes 16384
  181.9 4.2 %collective-permute-start.24 = (f32[2,2,2,128]{3,2,1,0:T(2,128)S(1)}, f32[2,2,2,128]{3,2,1,0:T(2,128)S(1)}, u32[]{:S(2)}, u32[]{:S(2)}) collective-permute-start(f32[2,2,2,128]{3,2,1,0:T(2,128)S(1)} %pad_maximum_fusion.47), channel_id=1, source_target_pairs={{0,16},{1,17},{2,18},{3,19},{4,20},{5,21},{6,22},{7,23},{8,24},{9,... | collective-permute-start | bytes 12296 | tf_op jit(solution)/shard_map/ppermute | solution.py:19
  187.4 4.2 %collective-permute-done.25 = f32[2,2,2,128]{3,2,1,0:T(2,128)S(1)} collective-permute-done((f32[2,2,2,128]{3,2,1,0:T(2,128)S(1)}, f32[2,2,2,128]{3,2,1,0:T(2,128)S(1)}, u32[]{:S(2)}, u32[]{:S(2)}) %collective-permute-start.25) | collective-permute-done | bytes 4128 | tf_op jit(solution)/shard_map/ppermute | solution.py:20
  194.3 3.9 collective-permute-done.27
  198.2 3.9 collective-permute-start.28
  203.8 4.2 %collective-permute-done.29 = f32[6,6,2,128]{3,2,1,0:T(2,128)S(1)} collective-permute-done((f32[6,6,2,128]{3,2,1,0:T(2,128)S(1)}, f32[6,6,2,128]{3,2,1,0:T(2,128)S(1)}, u32[]{:S(2)}, u32[]{:S(2)}) %collective-permute-start.29) | collective-permute-done | bytes 36896 | tf_op jit(solution)/shard_map/ppermute | solution.py:20
  211.5 4.2 %collective-permute-done.31 = f32[2,4,4,128]{3,2,1,0:T(4,128)S(1)} collective-permute-done((f32[2,4,4,128]{3,2,1,0:T(4,128)S(1)}, f32[2,4,4,128]{3,2,1,0:T(4,128)S(1)}, u32[]{:S(2)}, u32[]{:S(2)}) %collective-permute-start.31) | collective-permute-done | bytes 16416 | tf_op jit(solution)/shard_map/ppermute | solution.py:20
  218.6 4.2 %collective-permute-done.33 = f32[8,2,4,128]{3,2,1,0:T(4,128)S(1)} collective-permute-done((f32[8,2,4,128]{3,2,1,0:T(4,128)S(1)}, f32[8,2,4,128]{3,2,1,0:T(4,128)S(1)}, u32[]{:S(2)}, u32[]{:S(2)}) %collective-permute-start.33) | collective-permute-done | bytes 32800 | tf_op jit(solution)/shard_map/ppermute | solution.py:20
  222.9 2.6 collective-permute-start.34
  227.4 4.3 %collective-permute-done.35 = f32[8,8,2,128]{3,2,1,0:T(2,128)S(1)} collective-permute-done((f32[8,8,2,128]{3,2,1,0:T(2,128)S(1)}, f32[8,8,2,128]{3,2,1,0:T(2,128)S(1)}, u32[]{:S(2)}, u32[]{:S(2)}) %collective-permute-start.35) | collective-permute-done | bytes 65568 | tf_op jit(solution)/shard_map/ppermute | solution.py:20
  236.9 4.6 %collective-permute-done.37 = f32[2,8,8,128]{3,2,1,0:T(8,128)S(1)} collective-permute-done((f32[2,8,8,128]{3,2,1,0:T(8,128)S(1)}, f32[2,8,8,128]{3,2,1,0:T(8,128)S(1)}, u32[]{:S(2)}, u32[]{:S(2)}) %collective-permute-start.37) | collective-permute-done | bytes 65568 | tf_op jit(solution)/shard_map/ppermute | solution.py:20
  245.0 3.3 collective-permute-done.39
  253.1 4.4 %collective-permute-done.41 = f32[12,12,2,128]{3,2,1,0:T(2,128)S(1)} collective-permute-done((f32[12,12,2,128]{3,2,1,0:T(2,128)S(1)}, f32[12,12,2,128]{3,2,1,0:T(2,128)S(1)}, u32[]{:S(2)}, u32[]{:S(2)}) %collective-permute-start.41) | collective-permute-done | bytes 147488 | tf_op jit(solution)/shard_map/ppermute | solution.py:20
  265.1 4.5 %collective-permute-done.42 = f32[2,16,16,128]{3,2,1,0:T(8,128)S(1)} collective-permute-done((f32[2,16,16,128]{3,2,1,0:T(8,128)S(1)}, f32[2,16,16,128]{3,2,1,0:T(8,128)S(1)}, u32[]{:S(2)}, u32[]{:S(2)}) %collective-permute-start.42) | collective-permute-done | bytes 262176 | tf_op jit(solution)/shard_map/ppermute | solution.py:19
  269.6 4.7 %collective-permute-done.43 = f32[2,16,16,128]{3,2,1,0:T(8,128)S(1)} collective-permute-done((f32[2,16,16,128]{3,2,1,0:T(8,128)S(1)}, f32[2,16,16,128]{3,2,1,0:T(8,128)S(1)}, u32[]{:S(2)}, u32[]{:S(2)}) %collective-permute-start.43) | collective-permute-done | bytes 262176 | tf_op jit(solution)/shard_map/ppermute | solution.py:20
  275.0 2.3 collective-permute-start.44
  282.7 2.7 collective-permute-start.46
  286.9 2.8 reshape_reshape.3
  290.4 5.4 %collective-permute-done.47 = f32[20,20,2,128]{3,2,1,0:T(2,128)} collective-permute-done((f32[20,20,2,128]{3,2,1,0:T(2,128)}, f32[20,20,2,128]{3,2,1,0:T(2,128)}, u32[]{:S(2)}, u32[]{:S(2)}) %collective-permute-start.47) | collective-permute-done | bytes 409632 | tf_op jit(solution)/shard_map/ppermute | solution.py:20
  295.8 4.6 %fusion.11 = f32[20,20,20,128]{3,2,1,0:T(8,128)S(1)} fusion(f32[16,16,16,64]{3,2,1,0:T(8,128)S(1)} %reshape.351, f32[20,20,2,128]{3,2,1,0:T(2,128)} %collective-permute-done.47, f32[20,2,16,128]{3,2,1,0:T(8,128)S(1)} %collective-permute-done.45, f32[2,16,16,128]{3,2,1,0:T(8,128)S(1)} %collective-permute-done.43, f32[16,16,16,64]{3,2,1,0:T(8,128)} %copy-done.4, ...), kind=kLoop, calls=%fused_computation.13 | loop fusion | flops 7168000 | bytes 8192000 | tf_op jit(solution)/shard_map/concatenate | solution.py:21
  300.4 9.5 %fusion.35 = f32[18,18,18,64]{3,2,1,0:T(8,128)S(1)} fusion(f32[16,16,16,64]{3,2,1,0:T(8,128)S(1)} %reshape.351, f32[20,20,2,128]{3,2,1,0:T(2,128)} %collective-permute-done.46, f32[20,2,16,128]{3,2,1,0:T(8,128)S(1)} %collective-permute-done.45, f32[20,2,16,128]{3,2,1,0:T(8,128)S(1)} %collective-permute-done.44, ...), kind=kLoop, calls=%fused_computation.41 | loop fusion | flops 8584704 | bytes 14570272 | tf_op jit(solution)/shard_map/mul | solution.py:108
  309.9 3.1 fusion.61
  313.0 2.9 reshape.365
  315.9 5.2 %convolution_bitcast_fusion = f32[64,64]{0,1:T(8,128)S(1)} fusion(f32[4096,64]{1,0:T(8,128)S(1)} %bitcast.74, f32[4096,64]{1,0:T(8,128)} %reshape_reshape.3), kind=kOutput, calls=%fused_computation.108 | convolution fusion | flops 201326592 | bytes 2113536 | tf_op jit(solution)/shard_map/dot_general | solution.py:131
  321.1 72.9 %all-gather.1 = f32[2048,64]{1,0:T(8,128)S(1)} all-gather(f32[64,64]{1,0:T(8,128)S(1)} %copy.6), channel_id=3, replica_groups=mesh['gx'=2,'gy'=4,'gz'=4] {'gx','gy','gz'}, dimensions={0}, use_global_device_ids=true | all-gather | bytes 540672 | tf_op jit(solution)/shard_map/all_gather | solution.py:137
  (214 shorter events, 92.0 us)
Async XLA Ops:
  4.8 10.4 %collective-permute-start = (f32[2,16,16,128]{3,2,1,0:T(8,128)S(1)}, f32[2,16,16,128]{3,2,1,0:T(8,128)S(1)}, u32[]{:S(2)}, u32[]{:S(2)}) collective-permute-start(f32[2,16,16,128]{3,2,1,0:T(8,128)S(1)} %get-tuple-element.20), channel_id=1, source_target_pairs={{0,16},{1,17},{2,18},{3,19},{4,20},{5,21},{6,22},{7,23},{8,24},{9,... | collective-permute-start | bytes 786440 | tf_op jit(solution)/shard_map/ppermute | solution.py:19
  9.7 9.7 %collective-permute-start.1 = (f32[2,16,16,128]{3,2,1,0:T(8,128)S(1)}, f32[2,16,16,128]{3,2,1,0:T(8,128)S(1)}, u32[]{:S(2)}, u32[]{:S(2)}) collective-permute-start(f32[2,16,16,128]{3,2,1,0:T(8,128)S(1)} %get-tuple-element.8), channel_id=1, source_target_pairs={{16,0},{17,1},{18,2},{19,3},{20,4},{21,5},{22,6},{23,7},{24,8},{25... | collective-permute-start | bytes 786440 | tf_op jit(solution)/shard_map/ppermute | solution.py:20
  21.6 2.7 collective-permute-start.2
  22.9 5.2 %collective-permute-start.3 = (f32[20,2,16,128]{3,2,1,0:T(8,128)S(1)}, f32[20,2,16,128]{3,2,1,0:T(8,128)S(1)}, u32[]{:S(2)}, u32[]{:S(2)}) collective-permute-start(f32[20,2,16,128]{3,2,1,0:T(8,128)S(1)} %get-tuple-element.17), channel_id=1, source_target_pairs={{4,0},{8,4},{12,8},{5,1},{9,5},{13,9},{6,2},{10,6},{14,10},{7,3},{... | collective-permute-start | bytes 983048 | tf_op jit(solution)/shard_map/ppermute | solution.py:20
  29.2 8.9 %collective-permute-start.4 = (f32[20,20,2,128]{3,2,1,0:T(2,128)S(1)}, f32[20,20,2,128]{3,2,1,0:T(2,128)S(1)}, u32[]{:S(2)}, u32[]{:S(2)}) collective-permute-start(f32[20,20,2,128]{3,2,1,0:T(2,128)S(1)} %get-tuple-element.13), channel_id=1, source_target_pairs={{0,1},{1,2},{2,3},{4,5},{5,6},{6,7},{8,9},{9,10},{10,11},{12,13},{... | collective-permute-start | bytes 1228808 | tf_op jit(solution)/shard_map/ppermute | solution.py:19
  32.7 10.1 %collective-permute-start.5 = (f32[20,20,2,128]{3,2,1,0:T(2,128)S(1)}, f32[20,20,2,128]{3,2,1,0:T(2,128)S(1)}, u32[]{:S(2)}, u32[]{:S(2)}) collective-permute-start(f32[20,20,2,128]{3,2,1,0:T(2,128)S(1)} %get-tuple-element.12), channel_id=1, source_target_pairs={{1,0},{2,1},{3,2},{5,4},{6,5},{7,6},{9,8},{10,9},{11,10},{13,12},{... | collective-permute-start | bytes 1228808 | tf_op jit(solution)/shard_map/ppermute | solution.py:20
  61.1 3.5 collective-permute-start.6
  62.5 6.2 %collective-permute-start.7 = (f32[2,8,8,128]{3,2,1,0:T(8,128)S(1)}, f32[2,8,8,128]{3,2,1,0:T(8,128)S(1)}, u32[]{:S(2)}, u32[]{:S(2)}) collective-permute-start(f32[2,8,8,128]{3,2,1,0:T(8,128)S(1)} %get-tuple-element.6), channel_id=1, source_target_pairs={{16,0},{17,1},{18,2},{19,3},{20,4},{21,5},{22,6},{23,7},{24,8},{25... | collective-permute-start | bytes 196616 | tf_op jit(solution)/shard_map/ppermute | solution.py:20
  68.8 5.9 %collective-permute-start.8 = (f32[12,2,8,128]{3,2,1,0:T(8,128)S(1)}, f32[12,2,8,128]{3,2,1,0:T(8,128)S(1)}, u32[]{:S(2)}, u32[]{:S(2)}) collective-permute-start(f32[12,2,8,128]{3,2,1,0:T(8,128)S(1)} %get-tuple-element.27), channel_id=1, source_target_pairs={{0,4},{4,8},{8,12},{1,5},{5,9},{9,13},{2,6},{6,10},{10,14},{3,7},{... | collective-permute-start | bytes 294920 | tf_op jit(solution)/shard_map/ppermute | solution.py:19
  73.4 5.0 %collective-permute-start.9 = (f32[12,2,8,128]{3,2,1,0:T(8,128)S(1)}, f32[12,2,8,128]{3,2,1,0:T(8,128)S(1)}, u32[]{:S(2)}, u32[]{:S(2)}) collective-permute-start(f32[12,2,8,128]{3,2,1,0:T(8,128)S(1)} %get-tuple-element.28), channel_id=1, source_target_pairs={{4,0},{8,4},{12,8},{5,1},{9,5},{13,9},{6,2},{10,6},{14,10},{7,3},{... | collective-permute-start | bytes 294920 | tf_op jit(solution)/shard_map/ppermute | solution.py:20
  78.6 6.1 %collective-permute-start.10 = (f32[12,12,2,128]{3,2,1,0:T(2,128)S(1)}, f32[12,12,2,128]{3,2,1,0:T(2,128)S(1)}, u32[]{:S(2)}, u32[]{:S(2)}) collective-permute-start(f32[12,12,2,128]{3,2,1,0:T(2,128)S(1)} %get-tuple-element.24), channel_id=1, source_target_pairs={{0,1},{1,2},{2,3},{4,5},{5,6},{6,7},{8,9},{9,10},{10,11},{12,13},{... | collective-permute-start | bytes 442376 | tf_op jit(solution)/shard_map/ppermute | solution.py:19
  82.1 7.0 %collective-permute-start.11 = (f32[12,12,2,128]{3,2,1,0:T(2,128)S(1)}, f32[12,12,2,128]{3,2,1,0:T(2,128)S(1)}, u32[]{:S(2)}, u32[]{:S(2)}) collective-permute-start(f32[12,12,2,128]{3,2,1,0:T(2,128)S(1)} %get-tuple-element.23), channel_id=1, source_target_pairs={{1,0},{2,1},{3,2},{5,4},{6,5},{7,6},{9,8},{10,9},{11,10},{13,12},{... | collective-permute-start | bytes 442376 | tf_op jit(solution)/shard_map/ppermute | solution.py:20
  91.7 3.1 collective-permute-start.12
  93.2 5.6 %collective-permute-start.13 = (f32[2,4,4,128]{3,2,1,0:T(4,128)S(1)}, f32[2,4,4,128]{3,2,1,0:T(4,128)S(1)}, u32[]{:S(2)}, u32[]{:S(2)}) collective-permute-start(f32[2,4,4,128]{3,2,1,0:T(4,128)S(1)} %get-tuple-element.45), channel_id=1, source_target_pairs={{16,0},{17,1},{18,2},{19,3},{20,4},{21,5},{22,6},{23,7},{24,8},{25... | collective-permute-start | bytes 49160 | tf_op jit(solution)/shard_map/ppermute | solution.py:20
  99.0 3.7 collective-permute-start.14
  101.3 5.4 %collective-permute-start.15 = (f32[8,2,4,128]{3,2,1,0:T(4,128)S(1)}, f32[8,2,4,128]{3,2,1,0:T(4,128)S(1)}, u32[]{:S(2)}, u32[]{:S(2)}) collective-permute-start(f32[8,2,4,128]{3,2,1,0:T(4,128)S(1)} %get-tuple-element.43), channel_id=1, source_target_pairs={{4,0},{8,4},{12,8},{5,1},{9,5},{13,9},{6,2},{10,6},{14,10},{7,3},{... | collective-permute-start | bytes 98312 | tf_op jit(solution)/shard_map/ppermute | solution.py:20
  106.8 5.4 %collective-permute-start.16 = (f32[8,8,2,128]{3,2,1,0:T(2,128)S(1)}, f32[8,8,2,128]{3,2,1,0:T(2,128)S(1)}, u32[]{:S(2)}, u32[]{:S(2)}) collective-permute-start(f32[8,8,2,128]{3,2,1,0:T(2,128)S(1)} %get-tuple-element.37), channel_id=1, source_target_pairs={{0,1},{1,2},{2,3},{4,5},{5,6},{6,7},{8,9},{9,10},{10,11},{12,13},{... | collective-permute-start | bytes 196616 | tf_op jit(solution)/shard_map/ppermute | solution.py:19
  110.3 6.2 %collective-permute-start.17 = (f32[8,8,2,128]{3,2,1,0:T(2,128)S(1)}, f32[8,8,2,128]{3,2,1,0:T(2,128)S(1)}, u32[]{:S(2)}, u32[]{:S(2)}) collective-permute-start(f32[8,8,2,128]{3,2,1,0:T(2,128)S(1)} %get-tuple-element.36), channel_id=1, source_target_pairs={{1,0},{2,1},{3,2},{5,4},{6,5},{7,6},{9,8},{10,9},{11,10},{13,12},{... | collective-permute-start | bytes 196616 | tf_op jit(solution)/shard_map/ppermute | solution.py:20
  116.9 3.7 collective-permute-start.18
  118.6 5.5 %collective-permute-start.19 = (f32[2,2,2,128]{3,2,1,0:T(2,128)S(1)}, f32[2,2,2,128]{3,2,1,0:T(2,128)S(1)}, u32[]{:S(2)}, u32[]{:S(2)}) collective-permute-start(f32[2,2,2,128]{3,2,1,0:T(2,128)S(1)} %pad_maximum_fusion.46), channel_id=1, source_target_pairs={{16,0},{17,1},{18,2},{19,3},{20,4},{21,5},{22,6},{23,7},{24,8},{25... | collective-permute-start | bytes 12296 | tf_op jit(solution)/shard_map/ppermute | solution.py:20
  124.1 3.0 collective-permute-start.20
  125.8 5.4 %collective-permute-start.21 = (f32[6,2,2,128]{3,2,1,0:T(2,128)S(1)}, f32[6,2,2,128]{3,2,1,0:T(2,128)S(1)}, u32[]{:S(2)}, u32[]{:S(2)}) collective-permute-start(f32[6,2,2,128]{3,2,1,0:T(2,128)S(1)} %fusion.281), channel_id=1, source_target_pairs={{4,0},{8,4},{12,8},{5,1},{9,5},{13,9},{6,2},{10,6},{14,10},{7,3},{... | collective-permute-start | bytes 36872 | tf_op jit(solution)/shard_map/ppermute | solution.py:20
  131.9 3.8 collective-permute-start.22
  133.9 6.2 %collective-permute-start.23 = (f32[6,6,2,128]{3,2,1,0:T(2,128)}, f32[6,6,2,128]{3,2,1,0:T(2,128)}, u32[]{:S(2)}, u32[]{:S(2)}) collective-permute-start(f32[6,6,2,128]{3,2,1,0:T(2,128)} %fusion.211), channel_id=1, source_target_pairs={{1,0},{2,1},{3,2},{5,4},{6,5},{7,6},{9,8},{10,9},{11,10},{13,12},{... | collective-permute-start | bytes 110600 | tf_op jit(solution)/shard_map/ppermute | solution.py:20
  181.9 5.5 %collective-permute-start.24 = (f32[2,2,2,128]{3,2,1,0:T(2,128)S(1)}, f32[2,2,2,128]{3,2,1,0:T(2,128)S(1)}, u32[]{:S(2)}, u32[]{:S(2)}) collective-permute-start(f32[2,2,2,128]{3,2,1,0:T(2,128)S(1)} %pad_maximum_fusion.47), channel_id=1, source_target_pairs={{0,16},{1,17},{2,18},{3,19},{4,20},{5,21},{6,22},{7,23},{8,24},{9,... | collective-permute-start | bytes 12296 | tf_op jit(solution)/shard_map/ppermute | solution.py:19
  186.1 5.5 %collective-permute-start.25 = (f32[2,2,2,128]{3,2,1,0:T(2,128)S(1)}, f32[2,2,2,128]{3,2,1,0:T(2,128)S(1)}, u32[]{:S(2)}, u32[]{:S(2)}) collective-permute-start(f32[2,2,2,128]{3,2,1,0:T(2,128)S(1)} %pad_maximum_fusion.47), channel_id=1, source_target_pairs={{16,0},{17,1},{18,2},{19,3},{20,4},{21,5},{22,6},{23,7},{24,8},{25... | collective-permute-start | bytes 12296 | tf_op jit(solution)/shard_map/ppermute | solution.py:20
  191.7 2.6 collective-permute-start.26
  192.9 5.2 %collective-permute-start.27 = (f32[6,2,2,128]{3,2,1,0:T(2,128)S(1)}, f32[6,2,2,128]{3,2,1,0:T(2,128)S(1)}, u32[]{:S(2)}, u32[]{:S(2)}) collective-permute-start(f32[6,2,2,128]{3,2,1,0:T(2,128)S(1)} %fusion.283), channel_id=1, source_target_pairs={{4,0},{8,4},{12,8},{5,1},{9,5},{13,9},{6,2},{10,6},{14,10},{7,3},{... | collective-permute-start | bytes 36872 | tf_op jit(solution)/shard_map/ppermute | solution.py:20
  198.2 5.5 %collective-permute-start.28 = (f32[6,6,2,128]{3,2,1,0:T(2,128)S(1)}, f32[6,6,2,128]{3,2,1,0:T(2,128)S(1)}, u32[]{:S(2)}, u32[]{:S(2)}) collective-permute-start(f32[6,6,2,128]{3,2,1,0:T(2,128)S(1)} %fusion.215), channel_id=1, source_target_pairs={{0,1},{1,2},{2,3},{4,5},{5,6},{6,7},{8,9},{9,10},{10,11},{12,13},{... | collective-permute-start | bytes 110600 | tf_op jit(solution)/shard_map/ppermute | solution.py:19
  202.1 5.9 %collective-permute-start.29 = (f32[6,6,2,128]{3,2,1,0:T(2,128)S(1)}, f32[6,6,2,128]{3,2,1,0:T(2,128)S(1)}, u32[]{:S(2)}, u32[]{:S(2)}) collective-permute-start(f32[6,6,2,128]{3,2,1,0:T(2,128)S(1)} %fusion.215), channel_id=1, source_target_pairs={{1,0},{2,1},{3,2},{5,4},{6,5},{7,6},{9,8},{10,9},{11,10},{13,12},{... | collective-permute-start | bytes 110600 | tf_op jit(solution)/shard_map/ppermute | solution.py:20
  208.4 3.1 collective-permute-start.30
  210.0 5.6 %collective-permute-start.31 = (f32[2,4,4,128]{3,2,1,0:T(4,128)S(1)}, f32[2,4,4,128]{3,2,1,0:T(4,128)S(1)}, u32[]{:S(2)}, u32[]{:S(2)}) collective-permute-start(f32[2,4,4,128]{3,2,1,0:T(4,128)S(1)} %get-tuple-element.41), channel_id=1, source_target_pairs={{16,0},{17,1},{18,2},{19,3},{20,4},{21,5},{22,6},{23,7},{24,8},{25... | collective-permute-start | bytes 49160 | tf_op jit(solution)/shard_map/ppermute | solution.py:20
  215.8 2.8 collective-permute-start.32
  217.3 5.5 %collective-permute-start.33 = (f32[8,2,4,128]{3,2,1,0:T(4,128)S(1)}, f32[8,2,4,128]{3,2,1,0:T(4,128)S(1)}, u32[]{:S(2)}, u32[]{:S(2)}) collective-permute-start(f32[8,2,4,128]{3,2,1,0:T(4,128)S(1)} %get-tuple-element.39), channel_id=1, source_target_pairs={{4,0},{8,4},{12,8},{5,1},{9,5},{13,9},{6,2},{10,6},{14,10},{7,3},{... | collective-permute-start | bytes 98312 | tf_op jit(solution)/shard_map/ppermute | solution.py:20
  222.9 4.5 %collective-permute-start.34 = (f32[8,8,2,128]{3,2,1,0:T(2,128)S(1)}, f32[8,8,2,128]{3,2,1,0:T(2,128)S(1)}, u32[]{:S(2)}, u32[]{:S(2)}) collective-permute-start(f32[8,8,2,128]{3,2,1,0:T(2,128)S(1)} %get-tuple-element.35), channel_id=1, source_target_pairs={{0,1},{1,2},{2,3},{4,5},{5,6},{6,7},{8,9},{9,10},{10,11},{12,13},{... | collective-permute-start | bytes 196616 | tf_op jit(solution)/shard_map/ppermute | solution.py:19
  225.5 6.2 %collective-permute-start.35 = (f32[8,8,2,128]{3,2,1,0:T(2,128)S(1)}, f32[8,8,2,128]{3,2,1,0:T(2,128)S(1)}, u32[]{:S(2)}, u32[]{:S(2)}) collective-permute-start(f32[8,8,2,128]{3,2,1,0:T(2,128)S(1)} %get-tuple-element.34), channel_id=1, source_target_pairs={{1,0},{2,1},{3,2},{5,4},{6,5},{7,6},{9,8},{10,9},{11,10},{13,12},{... | collective-permute-start | bytes 196616 | tf_op jit(solution)/shard_map/ppermute | solution.py:20
  233.1 3.9 collective-permute-start.36
  234.7 6.8 %collective-permute-start.37 = (f32[2,8,8,128]{3,2,1,0:T(8,128)S(1)}, f32[2,8,8,128]{3,2,1,0:T(8,128)S(1)}, u32[]{:S(2)}, u32[]{:S(2)}) collective-permute-start(f32[2,8,8,128]{3,2,1,0:T(8,128)S(1)} %get-tuple-element.30), channel_id=1, source_target_pairs={{16,0},{17,1},{18,2},{19,3},{20,4},{21,5},{22,6},{23,7},{24,8},{25... | collective-permute-start | bytes 196616 | tf_op jit(solution)/shard_map/ppermute | solution.py:20
  241.7 3.3 collective-permute-start.38
  243.6 4.6 %collective-permute-start.39 = (f32[12,2,8,128]{3,2,1,0:T(8,128)S(1)}, f32[12,2,8,128]{3,2,1,0:T(8,128)S(1)}, u32[]{:S(2)}, u32[]{:S(2)}) collective-permute-start(f32[12,2,8,128]{3,2,1,0:T(8,128)S(1)} %get-tuple-element.26), channel_id=1, source_target_pairs={{4,0},{8,4},{12,8},{5,1},{9,5},{13,9},{6,2},{10,6},{14,10},{7,3},{... | collective-permute-start | bytes 294920 | tf_op jit(solution)/shard_map/ppermute | solution.py:20
  248.5 4.6 %collective-permute-start.40 = (f32[12,12,2,128]{3,2,1,0:T(2,128)S(1)}, f32[12,12,2,128]{3,2,1,0:T(2,128)S(1)}, u32[]{:S(2)}, u32[]{:S(2)}) collective-permute-start(f32[12,12,2,128]{3,2,1,0:T(2,128)S(1)} %get-tuple-element.22), channel_id=1, source_target_pairs={{0,1},{1,2},{2,3},{4,5},{5,6},{6,7},{8,9},{9,10},{10,11},{12,13},{... | collective-permute-start | bytes 442376 | tf_op jit(solution)/shard_map/ppermute | solution.py:19
  250.4 7.0 %collective-permute-start.41 = (f32[12,12,2,128]{3,2,1,0:T(2,128)S(1)}, f32[12,12,2,128]{3,2,1,0:T(2,128)S(1)}, u32[]{:S(2)}, u32[]{:S(2)}) collective-permute-start(f32[12,12,2,128]{3,2,1,0:T(2,128)S(1)} %get-tuple-element.21), channel_id=1, source_target_pairs={{1,0},{2,1},{3,2},{5,4},{6,5},{7,6},{9,8},{10,9},{11,10},{13,12},{... | collective-permute-start | bytes 442376 | tf_op jit(solution)/shard_map/ppermute | solution.py:20
  262.2 7.4 %collective-permute-start.42 = (f32[2,16,16,128]{3,2,1,0:T(8,128)S(1)}, f32[2,16,16,128]{3,2,1,0:T(8,128)S(1)}, u32[]{:S(2)}, u32[]{:S(2)}) collective-permute-start(f32[2,16,16,128]{3,2,1,0:T(8,128)S(1)} %get-tuple-element.18), channel_id=1, source_target_pairs={{0,16},{1,17},{2,18},{3,19},{4,20},{5,21},{6,22},{7,23},{8,24},{9,... | collective-permute-start | bytes 786440 | tf_op jit(solution)/shard_map/ppermute | solution.py:19
  263.8 10.5 %collective-permute-start.43 = (f32[2,16,16,128]{3,2,1,0:T(8,128)S(1)}, f32[2,16,16,128]{3,2,1,0:T(8,128)S(1)}, u32[]{:S(2)}, u32[]{:S(2)}) collective-permute-start(f32[2,16,16,128]{3,2,1,0:T(8,128)S(1)} %get-tuple-element.19), channel_id=1, source_target_pairs={{16,0},{17,1},{18,2},{19,3},{20,4},{21,5},{22,6},{23,7},{24,8},{25... | collective-permute-start | bytes 786440 | tf_op jit(solution)/shard_map/ppermute | solution.py:20
  275.0 3.6 collective-permute-start.44
  277.3 3.5 collective-permute-start.45
  282.7 7.7 %collective-permute-start.46 = (f32[20,20,2,128]{3,2,1,0:T(2,128)}, f32[20,20,2,128]{3,2,1,0:T(2,128)}, u32[]{:S(2)}, u32[]{:S(2)}) collective-permute-start(f32[20,20,2,128]{3,2,1,0:T(2,128)} %get-tuple-element.11), channel_id=1, source_target_pairs={{0,1},{1,2},{2,3},{4,5},{5,6},{6,7},{8,9},{9,10},{10,11},{12,13},{... | collective-permute-start | bytes 1228808 | tf_op jit(solution)/shard_map/ppermute | solution.py:19
  285.4 10.4 %collective-permute-start.47 = (f32[20,20,2,128]{3,2,1,0:T(2,128)}, f32[20,20,2,128]{3,2,1,0:T(2,128)}, u32[]{:S(2)}, u32[]{:S(2)}) collective-permute-start(f32[20,20,2,128]{3,2,1,0:T(2,128)} %get-tuple-element.10), channel_id=1, source_target_pairs={{1,0},{2,1},{3,2},{5,4},{6,5},{7,6},{9,8},{10,9},{11,10},{13,12},{... | collective-permute-start | bytes 1228808 | tf_op jit(solution)/shard_map/ppermute | solution.py:20
  (19 other events, 313.0 us)
